TPU v7x, 32 devices: a whole 2x2x4 slice. The times are simulated.
32 devices in a mesh: groups: 2 (over x), patch: 16 (over z, y, core).
Axes of the slice: x: 2, y: 2, z: 4, core: 2. Of those that a mesh axis runs over, the one named last changes fastest.
Arguments:
- latent: bfloat16 [4, 16, 64, 640], P('groups', 'patch'), parts along dimension 0, may hold values from -6 to 6
- stale_states: bfloat16 [4, 16, 64, 640], P('groups', 'patch'), parts along dimension 0, may hold values from -180 to 180
- stale_sums: float32 [2, 4, 16, 2, 16], P(None, 'groups', 'patch'), parts along dimension 1, as said below
- timestep: int32 [2], P('groups'), parts along dimension 0, may hold values from 0 to 999
- norm_gain: float32 [2, 640], replicated, may hold values from 0.25 to 1.75
- conv_weight: bfloat16 [3, 3, 640, 640], replicated, may hold values from -0.078125 to 0.078125
- time_weight: bfloat16 [320, 640], replicated, may hold values from -0.3125 to 0.3125
- qkv_weight: bfloat16 [3, 640, 640], replicated, may hold values from -0.4375 to 0.4375
- out_weight: bfloat16 [640, 640], replicated, may hold values from -0.25 to 0.25
Outputs:
- block_out: bfloat16 [4, 16, 64, 640], P('groups', 'patch'), parts along dimension 0
- next_states: bfloat16 [4, 16, 64, 640], P('groups', 'patch'), parts along dimension 0
- next_sums: float32 [2, 4, 16, 2, 16], P(None, 'groups', 'patch'), parts along dimension 1
There are 2 independent parts, one for each index of `groups`. A program takes and returns all parts, laid end to end along the dimension named above; an argument that names none is the same for every part. Nothing has to cross between parts.
Inputs may be any that keep to these rules, and one draw needn't show every extreme that they name: `stale_sums`: in every row and group the second entry is at least the square of the first divided by 2560, and more than that.
All inputs are finite; a program needn't handle non-finite values.
Results may differ from a plain program's by a relative error of at most 0.0158.
The roundings to bfloat16 on the way count: a program that leaves them out, or rounds other values in their place, can miss the bound.
Values may be sent and summed in bfloat16 or wider, within the bound.
A program may use at most 128 MiB of HBM per device.

v0:
```python
import functools
import math

import jax
import jax.numpy as jnp
from jax import lax
from jax.experimental import pallas as pl
from jax.experimental.pallas import tpu as pltpu
from jax.sharding import PartitionSpec as P

HEAD_DIM = 64
PACK = 4
EPS = 1e-05


def snake_width(mesh):
    try:
        axis = mesh.axis_names.index("patch")
        line = mesh.devices
        for other in range(line.ndim - 1, -1, -1):
            if other != axis:
                line = line.take(0, axis=other)
        rows = {tuple(d.coords)[1] for d in line.flat}
        return 2 if len(rows) == 2 and tuple(line.flat[2].coords)[1] != tuple(line.flat[0].coords)[1] else 1
    except Exception:
        return 1


def ring_pos(chip, chips, width):
    if width == 1:
        return chip
    long = chips // 2
    z, y = chip // 2, chip % 2
    return z * (1 - y) + (2 * long - 1 - z) * y


def ring_chip(pos, chips, width):
    if width == 1:
        return pos
    long = chips // 2
    y = pos // long
    z = pos * (1 - y) + (2 * long - 1 - pos) * y
    return z * 2 + y


def body(n, width, t_ref, lat_ref, stale_ref, ssum_ref, gain_ref, conv_hbm, time_hbm, qkv_hbm, out_hbm,
         block_ref, states_ref, nsums_ref,
         conv_w, time_w, qkv_w, out_w, halo, sums_all, sums_out, rx, keys, values, act, q_s, att_s,
         w_sem, small_sem, ring_send, ring_recv, core_send, core_recv, halo_send, halo_recv, sum_send, sum_recv):
    images, _, columns, channels = lat_ref.shape
    groups = ssum_ref.shape[-1]
    f32, bf16 = jnp.float32, jnp.bfloat16
    tokens = images * columns
    chips, last = n // 2, n // 4
    half = images // 2
    count = float(n * columns * (channels // groups))
    me = lax.axis_index("patch")
    core = me % 2
    pos = ring_pos(me // 2, chips, width)
    ahead = ring_chip((pos + 1) % chips, chips, width) * 2 + core
    behind = ring_chip((pos + chips - 1) % chips, chips, width) * 2 + core
    sibling = me + 1 - 2 * core
    MESH = pl.DeviceIdType.MESH

    def load(src, dst, index):
        return pltpu.make_async_copy(src, dst, w_sem.at[index])

    conv_loads = [[load(conv_hbm.at[a, c], conv_w.at[a, c], 3 * a + c) for c in range(3)] for a in range(3)]
    time_load = load(time_hbm, time_w, 9)
    qkv_loads = [load(qkv_hbm.at[i], qkv_w.at[i], 10 + i) for i in range(3)]
    out_load = load(out_hbm, out_w, 13)
    own_sums = pltpu.make_async_copy(ssum_ref, sums_all.at[0], small_sem.at[0])
    own_sums.start()
    time_load.start()
    for c in range(3):
        for a in (1, 0, 2):
            conv_loads[a][c].start()
    for i in (1, 2, 0):
        qkv_loads[i].start()
    out_load.start()

    barrier = pltpu.get_barrier_semaphore()

    @pl.loop(1, n)
    def _(d):
        pl.semaphore_signal(barrier, inc=1, device_id={"patch": (me + d) % n}, device_id_type=MESH)

    pl.semaphore_wait(barrier, n - 1)

    def remote(src, dst, send, recv, target):
        return pltpu.make_async_remote_copy(src_ref=src, dst_ref=dst, send_sem=send, recv_sem=recv,
                                            device_id={"patch": target}, device_id_type=MESH)

    def sum_copy(d):
        return remote(sums_all.at[0], sums_all.at[d], sum_send.at[d], sum_recv.at[d], (me + d) % n)

    def halo_copy(slot):
        target = (me + 1) % n if slot == 0 else (me + n - 1) % n
        return remote(lat_ref, halo.at[slot], halo_send.at[slot], halo_recv.at[slot], target)

    def slot_of(step, direction):
        return 2 + 4 * (step - 1) + 2 * direction

    final_slot = 2 + 4 * (last - 1)

    def ring_copy(step, direction, image, first=False, final=False):
        src = stale_ref.at[image, 0] if first else rx.at[image, slot_of(step - 1, direction)]
        dst = rx.at[image, final_slot if final else slot_of(step, direction)]
        sems = (direction, step, image)
        return remote(src, dst, ring_send.at[sems], ring_recv.at[sems], ahead if direction == 0 else behind)

    def core_copy(slot, image):
        return remote(rx.at[image, slot], rx.at[image, slot + 1], core_send.at[slot, image],
                      core_recv.at[slot, image], sibling)

    def own_core_copy(image):
        return remote(stale_ref.at[image, 0], rx.at[image, 1], core_send.at[0, image],
                      core_recv.at[0, image], sibling)

    def final_direction(image):
        return 0 if image < half else 1

    own_sums.wait()

    @pl.loop(1, n)
    def _(d):
        sum_copy(d).start()

    @pl.when(me < n - 1)
    def _():
        halo_copy(0).start()

    @pl.when(me > 0)
    def _():
        halo_copy(1).start()

    order = [(i, d) for i in range(images) for d in ((0, 1) if i < half else (1, 0))]
    for image, direction in order:
        ring_copy(1, direction, image, first=True).start()
    for image in range(images):
        own_core_copy(image).start()

    @pl.when(me == 0)
    def _():
        halo[0] = jnp.zeros_like(lat_ref)

    @pl.when(me == n - 1)
    def _():
        halo[1] = jnp.zeros_like(lat_ref)

    def forward(step):
        for image, direction in order:
            ring_copy(step, direction, image, first=True).wait_recv()
            ring_copy(step + 1, direction, image).start()
            core_copy(slot_of(step, direction), image).start()

    def forward_last():
        for image, direction in order:
            ring_copy(last - 1, direction, image, first=True).wait_recv()
            if final_direction(image) == direction:
                ring_copy(last, direction, image, final=True).start()
            core_copy(slot_of(last - 1, direction), image).start()

    def project_rows(image, start, size):
        rows = rx[image, pl.ds(start, size)].reshape(size * columns, channels)
        for which, dest in ((1, keys), (2, values)):
            made = jnp.dot(rows, qkv_w[which], preferred_element_type=f32).astype(bf16)
            dest[image, pl.ds(start, size)] = made.reshape(size, columns, channels)

    def project(step):
        for image in range(images):
            for direction in range(2):
                core_copy(slot_of(step, direction), image).wait_recv()
            project_rows(image, slot_of(step, 0), 4)

    ch = lax.broadcasted_iota(jnp.int32, (channels, groups), 0)
    gr = lax.broadcasted_iota(jnp.int32, (channels, groups), 1) * (channels // groups)
    member = jnp.where((ch >= gr) & (ch < gr + channels // groups), 1.0, 0.0).astype(f32)
    ch_t = lax.broadcasted_iota(jnp.int32, (groups, channels), 1)
    gr_t = lax.broadcasted_iota(jnp.int32, (groups, channels), 0) * (channels // groups)
    member_t = jnp.where((ch_t >= gr_t) & (ch_t < gr_t + channels // groups), 1.0, 0.0).astype(f32)
    exact = functools.partial(jnp.dot, precision=lax.Precision.HIGHEST, preferred_element_type=f32)

    freq_count = time_w.shape[0] // 2
    idx = lax.broadcasted_iota(jnp.int32, (8, 2 * freq_count), 1)
    low = idx < freq_count
    freqs = jnp.exp(-math.log(10000.0) * jnp.where(low, idx, idx - freq_count).astype(f32) / freq_count)
    angles = t_ref[0].astype(f32) * freqs
    emb = jnp.where(low, jnp.cos(angles), jnp.sin(angles))
    emb = emb / (1.0 + jnp.exp(-emb))
    e_hi = emb.astype(bf16)
    rest = emb - e_hi.astype(f32)
    e_mid = rest.astype(bf16)
    e_lo = (rest - e_mid.astype(f32)).astype(bf16)
    time_load.wait()
    parts = [jnp.dot(e, time_w[...], preferred_element_type=f32) for e in (e_hi, e_mid, e_lo)]
    temb = (parts[2] + parts[1] + parts[0])[0:1]

    @pl.loop(1, n)
    def _(d):
        sum_copy(d).wait_recv()

    total = sums_all[0]
    total = lax.fori_loop(1, n, lambda d, acc: acc + sums_all[d], total)
    others = [total - sums_all[1], total - sums_all[0], total - sums_all[n - 1]]

    @pl.when(me > 0)
    def _():
        halo_copy(0).wait_recv()

    @pl.when(me < n - 1)
    def _():
        halo_copy(1).wait_recv()

    if last > 2:
        forward(1)

    def stacked(rows, size):
        pad = size - len(rows)
        if pad:
            rows = rows + [jnp.zeros((pad, rows[0].shape[1]), f32)]
        return jnp.concatenate(rows, axis=0)

    def statistics(blocks, norm, others_of):
        size = -(-len(blocks) // 8) * 8
        firsts = stacked([jnp.sum(x, axis=0, keepdims=True) for x in blocks], size)
        seconds = stacked([jnp.sum(x * x, axis=0, keepdims=True) for x in blocks], size)
        fresh = exact(jnp.concatenate([firsts, seconds], axis=0), member)
        fresh1, fresh2 = fresh[:size], fresh[size:]
        one = stacked([o[norm, b, 0, 0:1] for o, b in others_of], size)
        two = stacked([o[norm, b, 0, 1:2] for o, b in others_of], size)
        m = (one + fresh1) / count
        v = (two + fresh2) / count - m * m
        inv = lax.rsqrt(v + EPS)
        wide = exact(jnp.concatenate([m, inv], axis=0), member_t)
        return fresh1, fresh2, wide[:size], wide[size:]

    def widened(row, image):
        src = lat_ref[image, 0] if row == 1 else halo[0 if row == 0 else 1, image, 0]
        return src.astype(f32)

    pairs = [(r, b) for r in range(3) for b in range(images)]
    fresh1, fresh2, mean, inv = statistics([widened(r, b) for r, b in pairs], 0, [(others[r], b) for r, b in pairs])
    for b in range(images):
        i = images + b
        sums_out[0, b, 0, 0:1] = fresh1[i : i + 1]
        sums_out[0, b, 0, 1:2] = fresh2[i : i + 1]
    inside = [jnp.where(me > 0, 1.0, 0.0).astype(f32), None, jnp.where(me < n - 1, 1.0, 0.0).astype(f32)]
    for i, (r, b) in enumerate(pairs):
        u = (widened(r, b) - mean[i : i + 1]) * inv[i : i + 1] * gain_ref[0:1, :]
        u = u / (1.0 + jnp.exp(-u))
        if inside[r] is not None:
            u = u * inside[r]
        act[r, pl.ds(b * columns, columns)] = u.astype(bf16)

    def tap(c):
        acc = None
        for a in (1, 0, 2):
            conv_loads[a][c].wait()
            part = jnp.dot(act[a], conv_w[a, c], preferred_element_type=f32)
            acc = part if acc is None else acc + part
        return acc

    place = lax.broadcasted_iota(jnp.int32, (tokens, channels), 0)
    first_col = place == 0
    last_col = place == columns - 1
    for b in range(1, images):
        first_col = first_col | (place == b * columns)
        last_col = last_col | (place == (b + 1) * columns - 1)
    left = jnp.where(first_col, 0.0, pltpu.roll(tap(0), 1, 0))
    conv = left + tap(1)
    if last > 3:
        forward(2)
    conv = conv + jnp.where(last_col, 0.0, pltpu.roll(tap(2), tokens - 1, 0))
    lat = jnp.concatenate([widened(1, b) for b in range(images)], axis=0)
    hidden = (lat + conv + temb).astype(bf16)
    wide_hidden = hidden.astype(f32)
    blocks = [wide_hidden[b * columns : (b + 1) * columns] for b in range(images)]
    fresh1, fresh2, mean, inv = statistics(blocks, 1, [(others[1], b) for b in range(images)])
    normed = []
    for b in range(images):
        sums_out[1, b, 0, 0:1] = fresh1[b : b + 1]
        sums_out[1, b, 0, 1:2] = fresh2[b : b + 1]
        s = ((blocks[b] - mean[b : b + 1]) * inv[b : b + 1] * gain_ref[1:2, :]).astype(bf16)
        states_ref[b, 0] = s
        normed.append(s)
    states = jnp.concatenate(normed, axis=0)
    store_sums = pltpu.make_async_copy(sums_out.at[pl.ds(0, 2)], nsums_ref, small_sem.at[1])
    store_sums.start()

    for load_ in qkv_loads:
        load_.wait()
    q_s[...] = jnp.dot(states, qkv_w[0], preferred_element_type=f32).astype(bf16)
    for which, dest in ((1, keys), (2, values)):
        made = jnp.dot(states, qkv_w[which], preferred_element_type=f32).astype(bf16)
        for b in range(images):
            dest[b, 0] = made[b * columns : (b + 1) * columns]
    for image in range(images):
        own_core_copy(image).wait_recv()
        project_rows(image, 1, 1)

    done = min(2, last - 2)
    project(1)
    if last - 1 > done + 1:
        @pl.loop(done + 1, last - 1)
        def _(step):
            forward(step)
            project(step - 1)
    forward_last()
    for step in range(max(2, last - 2 if last - 1 > done + 1 else 2), last):
        project(step)
    for image in range(images):
        ring_copy(last, final_direction(image), image, final=True).wait_recv()
        core_copy(final_slot, image).start()
    for image in range(images):
        core_copy(final_slot, image).wait_recv()
        project_rows(image, final_slot, 2)

    factor = math.log2(math.e) / math.sqrt(HEAD_DIM)
    total_keys = n * columns
    for b in range(images):
        for c0 in range(0, channels, PACK * HEAD_DIM):
            c1 = min(c0 + PACK * HEAD_DIM, channels)
            heads = (c1 - c0) // HEAD_DIM
            qt = q_s[pl.ds(b * columns, columns), c0:c1]
            lane = lax.broadcasted_iota(jnp.int32, (columns, c1 - c0), 1)
            own = [(lane >= h * HEAD_DIM) & (lane < (h + 1) * HEAD_DIM) for h in range(heads)]
            qb = jnp.concatenate([jnp.where(own[h], qt, jnp.zeros_like(qt)) for h in range(heads)], axis=0)
            kk = keys[b, :, :, c0:c1].reshape(total_keys, c1 - c0)
            vv = values[b, :, :, c0:c1].reshape(total_keys, c1 - c0)
            s = lax.dot_general(qb, kk, (((1,), (1,)), ((), ())), preferred_element_type=f32)
            e = jnp.exp2((s - jnp.max(s, axis=1, keepdims=True)) * factor)
            den = jnp.sum(e, axis=1, keepdims=True)
            o = jnp.dot(e.astype(bf16), vv, preferred_element_type=f32) / den
            mixed = jnp.where(own[0], o[0:columns], 0.0)
            for h in range(1, heads):
                mixed = mixed + jnp.where(own[h], o[h * columns : (h + 1) * columns], 0.0)
            att_s[pl.ds(b * columns, columns), c0:c1] = mixed.astype(bf16)

    out_load.wait()
    result = wide_hidden + jnp.dot(att_s[...], out_w[...], preferred_element_type=f32)
    for b in range(images):
        block_ref[b, 0] = result[b * columns : (b + 1) * columns].astype(bf16)

    store_sums.wait()

    @pl.loop(1, n)
    def _(d):
        sum_copy(d).wait_send()

    @pl.when(me < n - 1)
    def _():
        halo_copy(0).wait_send()

    @pl.when(me > 0)
    def _():
        halo_copy(1).wait_send()

    for image in range(images):
        own_core_copy(image).wait_send()
        for direction in range(2):
            ring_copy(1, direction, image, first=True).wait_send()

            @pl.loop(2, last)
            def _(step):
                ring_copy(step, direction, image).wait_send()

            @pl.loop(1, last)
            def _(step):
                core_copy(slot_of(step, direction), image).wait_send()

        ring_copy(last, final_direction(image), image, final=True).wait_send()
        core_copy(final_slot, image).wait_send()


def settle(block_in, states_in, sums_in, block_ref, states_ref, sums_ref, sem):
    copies = [
        pltpu.make_async_copy(src, dst, sem.at[i])
        for i, (src, dst) in enumerate(((block_in, block_ref), (states_in, states_ref), (sums_in, sums_ref)))
    ]
    for copy in copies:
        copy.start()
    for copy in copies:
        copy.wait()


def solution(mesh):
    n = mesh.shape["patch"]
    width = snake_width(mesh)

    def local(latent, stale_states, stale_sums, timestep, norm_gain, conv_weight, time_weight, qkv_weight, out_weight):
        images, row_count, columns, channels = latent.shape
        assert row_count == 1 and n % 4 == 0 and n >= 8 and images % 2 == 0
        vmem = pl.BlockSpec(memory_space=pltpu.VMEM)
        anywhere = pl.BlockSpec(memory_space=pl.ANY)
        bf16 = jnp.bfloat16
        dma = pltpu.SemaphoreType.DMA
        steps = n // 4 + 1
        made = pl.pallas_call(
            functools.partial(body, n, width),
            out_shape=(
                jax.ShapeDtypeStruct(latent.shape, bf16),
                jax.ShapeDtypeStruct(latent.shape, bf16),
                jax.ShapeDtypeStruct(stale_sums.shape, jnp.float32),
            ),
            in_specs=[pl.BlockSpec(memory_space=pltpu.SMEM)] + [vmem, vmem, anywhere, vmem] + [anywhere] * 4,
            out_specs=(vmem, vmem, anywhere),
            scratch_shapes=[
                pltpu.VMEM(conv_weight.shape, bf16),
                pltpu.VMEM(time_weight.shape, bf16),
                pltpu.VMEM(qkv_weight.shape, bf16),
                pltpu.VMEM(out_weight.shape, bf16),
                pltpu.VMEM((2,) + latent.shape, bf16),
                pltpu.VMEM((n + 1,) + stale_sums.shape, jnp.float32),
                pltpu.VMEM((3,) + stale_sums.shape[1:], jnp.float32),
                pltpu.VMEM((images, n, columns, channels), bf16),
                pltpu.VMEM((images, n, columns, channels), bf16),
                pltpu.VMEM((images, n, columns, channels), bf16),
                pltpu.VMEM((3, images * columns, channels), bf16),
                pltpu.VMEM((images * columns, channels), bf16),
                pltpu.VMEM((images * columns, channels), bf16),
                dma((14,)),
                dma((2,)),
                dma((2, steps, images)),
                dma((2, steps, images)),
                dma((n, images)),
                dma((n, images)),
                dma((2,)),
                dma((2,)),
                dma((n,)),
                dma((n,)),
            ],
            compiler_params=pltpu.CompilerParams(
                collective_id=0, has_side_effects=True, vmem_limit_bytes=60 * 1024 * 1024
            ),
        )(timestep, latent, stale_states, stale_sums, norm_gain, conv_weight, time_weight, qkv_weight, out_weight)
        return pl.pallas_call(
            settle,
            out_shape=tuple(jax.ShapeDtypeStruct(x.shape, x.dtype) for x in made),
            in_specs=[vmem] * 3,
            out_specs=(anywhere,) * 3,
            scratch_shapes=[dma((3,))],
        )(*made)

    in_specs = (
        P("groups", "patch", None, None),
        P("groups", "patch", None, None),
        P(None, "groups", "patch", None, None),
        P("groups"),
        P(),
        P(),
        P(),
        P(),
        P(),
    )
    out_specs = (
        P("groups", "patch", None, None),
        P("groups", "patch", None, None),
        P(None, "groups", "patch", None, None),
    )
    return jax.shard_map(local, mesh=mesh, in_specs=in_specs, out_specs=out_specs, check_vma=False)
```

profile of v0, /device:TPU:1, one launch (start us, length us, event | category | flops | bytes accessed | tf_op | source)
XLA Modules:
  0.0 38.1 jit_solution(14472572793995168862)
XLA Ops:
  1.3 35.1 %shard_map.112 = (bf16[2,1,64,640]{3,2,1,0:T(8,128)(2,1)}, bf16[2,1,64,640]{3,2,1,0:T(8,128)(2,1)}, f32[2,2,1,2,16]{4,3,2,1,0:T(2,128)}) custom-call(s32[1]{0:T(128)S(6)} %copy.12.t_ref, bf16[2,1,64,640]{3,2,1,0:T(8,128)(2,1)} %lat_ref.1, bf16[2,1,64,640]{3,2,1,0:T(8,128)(2,1)} %stale_ref.1, f32[2,2,1,2,16]{4,3,2,1,0:T(2,128)} %ssum_ref.1, ...), custom_call_target="tpu_custom_call" | custom-call | tf_op jit(solution)/shard_map/pallas_call | solution.py:399
  36.4 1.7 %shard_map.113 = (bf16[2,1,64,640]{3,2,1,0:T(8,128)(2,1)}, bf16[2,1,64,640]{3,2,1,0:T(8,128)(2,1)}, f32[2,2,1,2,16]{4,3,2,1,0:T(2,128)}) custom-call(bf16[2,1,64,640]{3,2,1,0:T(8,128)(2,1)} %get-tuple-element.6.block_in, bf16[2,1,64,640]{3,2,1,0:T(8,128)(2,1)} %get-tuple-element.7.states_in, f32[2,2,1,2,16]{4,3,2,1,0:T(2,128)} %get-tuple-element.8.sums_in), custom_call_target="tpu_custom_call" | custom-call | tf_op jit(solution)/shard_map/pallas_call | solution.py:437
where the time goes:
time: 38.3 us; the launch traced here: 38.1 us
  Pallas kernels  36.8 us (96%)
  between operations  1.29 us (3%)
    pallas_call x1, Pallas kernels, local(): pl.pallas_call(functools.partial(body, n, width), out_shape=(jax.ShapeDty...  35.1 us
    pallas_call x1, Pallas kernels, local(): pl.pallas_call(settle, out_shape=tuple((jax.ShapeDtypeStruct(x.shape, x.d...  1.74 us

commit v1 on v0

v1 whole, which is shorter than its diff:
```python
import functools
import math

import jax
import jax.numpy as jnp
from jax import lax
from jax.experimental import pallas as pl
from jax.experimental.pallas import tpu as pltpu
from jax.sharding import PartitionSpec as P

HEAD_DIM = 64
PACK = 4
EPS = 1e-05


def snake_width(mesh):
    try:
        axis = mesh.axis_names.index("patch")
        line = mesh.devices
        for other in range(line.ndim - 1, -1, -1):
            if other != axis:
                line = line.take(0, axis=other)
        rows = {tuple(d.coords)[1] for d in line.flat}
        return 2 if len(rows) == 2 and tuple(line.flat[2].coords)[1] != tuple(line.flat[0].coords)[1] else 1
    except Exception:
        return 1


def ring_pos(chip, chips, width):
    if width == 1:
        return chip
    long = chips // 2
    z, y = chip // 2, chip % 2
    return z * (1 - y) + (2 * long - 1 - z) * y


def ring_chip(pos, chips, width):
    if width == 1:
        return pos
    long = chips // 2
    y = pos // long
    z = pos * (1 - y) + (2 * long - 1 - pos) * y
    return z * 2 + y


def body(n, width, t_hbm, lat_hbm, stale_hbm, ssum_hbm, gain_hbm, conv_hbm, time_hbm, qkv_hbm, out_hbm,
         block_ref, states_ref, nsums_ref,
         t_ref, lat_ref, stale_ref, gain_ref, conv_w, time_w, qkv_w, out_w, halo, sums_all, sums_out, rx, keys, values,
         act, q_s, att_s, max_s, den_s, mix_s,
         w_sem, small_sem, ring_send, ring_recv, core_send, core_recv, halo_send, halo_recv, sum_send, sum_recv):
    images, _, columns, channels = lat_ref.shape
    groups = ssum_hbm.shape[-1]
    f32, bf16 = jnp.float32, jnp.bfloat16
    tokens = images * columns
    chips, last = n // 2, n // 4
    count = float(n * columns * (channels // groups))
    me = lax.axis_index("patch")
    core = me % 2
    pos = ring_pos(me // 2, chips, width)
    ahead = ring_chip((pos + 1) % chips, chips, width) * 2
    behind = ring_chip((pos + chips - 1) % chips, chips, width) * 2
    target = ahead * (1 - core) + behind * core + core
    sibling = me + 1 - 2 * core
    MESH = pl.DeviceIdType.MESH

    barrier = pltpu.get_barrier_semaphore()

    @pl.loop(1, n)
    def _(d):
        pl.semaphore_signal(barrier, inc=1, device_id={"patch": (me + d) % n}, device_id_type=MESH)

    def load(src, dst, index):
        return pltpu.make_async_copy(src, dst, w_sem.at[index])

    conv_loads = [[load(conv_hbm.at[a, c], conv_w.at[a, c], 3 * a + c) for c in range(3)] for a in range(3)]
    time_load = load(time_hbm, time_w, 9)
    qkv_loads = [load(qkv_hbm.at[i], qkv_w.at[i], 10 + i) for i in range(3)]
    out_load = load(out_hbm, out_w, 13)
    small = [
        pltpu.make_async_copy(src, dst, small_sem.at[i])
        for i, (src, dst) in enumerate(
            ((stale_hbm, stale_ref), (ssum_hbm, sums_all.at[0]), (lat_hbm, lat_ref), (t_hbm, t_ref), (gain_hbm, gain_ref))
        )
    ]
    for copy in small:
        copy.start()
    time_load.start()
    for c in range(3):
        for a in (1, 0, 2):
            conv_loads[a][c].start()
    for i in (0, 1, 2):
        qkv_loads[i].start()
    out_load.start()

    def remote(src, dst, send, recv, where):
        return pltpu.make_async_remote_copy(src_ref=src, dst_ref=dst, send_sem=send, recv_sem=recv,
                                            device_id={"patch": where}, device_id_type=MESH)

    def sum_copy(d):
        return remote(sums_all.at[0], sums_all.at[d], sum_send.at[d], sum_recv.at[d], (me + d) % n)

    def halo_copy(slot):
        where = (me + 1) % n if slot == 0 else (me + n - 1) % n
        return remote(lat_ref, halo.at[slot], halo_send.at[slot], halo_recv.at[slot], where)

    def slot_of(step, direction, row, final):
        return 2 + 4 * (step - 1) + row + (0 if final else 2 * direction)

    def chunk(i, direction):
        return (direction if i < images else 1 - direction), i % images

    def ring_copy(step, i, first=False, final=False):
        row, image = chunk(i, core)
        if first:
            src = stale_ref.at[image, 0] if i < images else rx.at[image, 1]
        else:
            src = rx.at[image, slot_of(step - 1, core, row, False)]
        return remote(src, rx.at[image, slot_of(step, core, row, final)],
                      ring_send.at[step, i], ring_recv.at[step, i], target)

    def core_copy(step, i, final=False, direction=None):
        direction = core if direction is None else direction
        row, image = chunk(i, direction)
        ref = rx.at[image, slot_of(step, direction, row, final)]
        return remote(ref, ref, core_send.at[step, i], core_recv.at[step, i], sibling)

    def own_core_copy(image):
        return remote(stale_ref.at[image, 0], rx.at[image, 1], core_send.at[0, image],
                      core_recv.at[0, image], sibling)

    small[0].wait()
    small[1].wait()
    small[2].wait()
    pl.semaphore_wait(barrier, n - 1)

    for image in range(images):
        own_core_copy(image).start()

    @pl.loop(1, n)
    def _(d):
        sum_copy(d).start()

    for image in range(images):
        ring_copy(1, image, first=True).start()

    @pl.when(me < n - 1)
    def _():
        halo_copy(0).start()

    @pl.when(me > 0)
    def _():
        halo_copy(1).start()

    for image in range(images):
        own_core_copy(image).wait_recv()
        ring_copy(1, images + image, first=True).start()

    def event(step, i, kind):
        ring_copy(step, i, first=True, final=kind == 2).wait_recv()
        if kind == 0 or (kind == 1 and i < images):
            ring_copy(step + 1, i, final=kind == 1).start()
        core_copy(step, i, final=kind == 2).start()

    def count_of(kind):
        return images if kind == 2 else 2 * images

    def kind_of(step):
        return 2 if step == last else 1 if step == last - 1 else 0

    static = [s for s in range(1, last + 1) if last <= 4 or s <= 2]
    queue = [(s, i, kind_of(s)) for s in static for i in range(count_of(kind_of(s)))]

    def pump(amount=1):
        for _ in range(min(amount, len(queue))):
            event(*queue.pop(0))

    def drain(step):
        while queue and queue[0][0] <= step:
            pump()

    def forward(step, kind):
        for i in range(count_of(kind)):
            event(step, i, kind)

    @pl.when(me == 0)
    def _():
        halo[0] = jnp.zeros_like(lat_ref)

    @pl.when(me == n - 1)
    def _():
        halo[1] = jnp.zeros_like(lat_ref)

    def project_rows(image, start, size):
        rows = rx[image, pl.ds(start, size)].reshape(size * columns, channels)
        for which, dest in ((1, keys), (2, values)):
            made = jnp.dot(rows, qkv_w[which], preferred_element_type=f32).astype(bf16)
            dest[image, pl.ds(start, size)] = made.reshape(size, columns, channels)

    def arrived(step, kind):
        for i in range(count_of(kind)):
            core_copy(step, i, final=kind == 2, direction=1 - core).wait_recv()

    def project(step, kind, between=None):
        arrived(step, kind)
        for image in range(images):
            project_rows(image, slot_of(step, 0, 0, kind == 2), 2 if kind == 2 else 4)
            if between is not None:
                between()

    ch = lax.broadcasted_iota(jnp.int32, (channels, groups), 0)
    gr = lax.broadcasted_iota(jnp.int32, (channels, groups), 1) * (channels // groups)
    member = jnp.where((ch >= gr) & (ch < gr + channels // groups), 1.0, 0.0).astype(bf16)
    ch_t = lax.broadcasted_iota(jnp.int32, (groups, channels), 1)
    gr_t = lax.broadcasted_iota(jnp.int32, (groups, channels), 0) * (channels // groups)
    member_t = jnp.where((ch_t >= gr_t) & (ch_t < gr_t + channels // groups), 1.0, 0.0).astype(bf16)

    def exact(x, picks):
        rows = x.shape[0]
        hi = x.astype(bf16)
        rest = x - hi.astype(f32)
        mid = rest.astype(bf16)
        lo = (rest - mid.astype(f32)).astype(bf16)
        y = jnp.dot(jnp.concatenate([hi, mid, lo], axis=0), picks, preferred_element_type=f32)
        return y[2 * rows :] + y[rows : 2 * rows] + y[:rows]

    freq_count = time_w.shape[0] // 2
    idx = lax.broadcasted_iota(jnp.int32, (8, 2 * freq_count), 1)
    low = idx < freq_count
    freqs = jnp.exp(-math.log(10000.0) * jnp.where(low, idx, idx - freq_count).astype(f32) / freq_count)
    small[3].wait()
    small[4].wait()
    angles = t_ref[0].astype(f32) * freqs
    emb = jnp.where(low, jnp.cos(angles), jnp.sin(angles))
    emb = emb / (1.0 + jnp.exp(-emb))
    time_load.wait()
    temb = exact(emb, time_w[...])[0:1]

    pump(2)

    @pl.loop(1, n)
    def _(d):
        sum_copy(d).wait_recv()

    total = sums_all[0]
    total = lax.fori_loop(1, n, lambda d, acc: acc + sums_all[d], total)
    others = [total - sums_all[1], total - sums_all[0], total - sums_all[n - 1]]

    @pl.when(me > 0)
    def _():
        halo_copy(0).wait_recv()

    @pl.when(me < n - 1)
    def _():
        halo_copy(1).wait_recv()

    pump(1)

    def stacked(rows, size):
        pad = size - len(rows)
        if pad:
            rows = rows + [jnp.zeros((pad, rows[0].shape[1]), f32)]
        return jnp.concatenate(rows, axis=0)

    def statistics(blocks, norm, others_of):
        size = -(-len(blocks) // 8) * 8
        firsts = stacked([jnp.sum(x, axis=0, keepdims=True) for x in blocks], size)
        seconds = stacked([jnp.sum(x * x, axis=0, keepdims=True) for x in blocks], size)
        fresh = exact(jnp.concatenate([firsts, seconds], axis=0), member)
        fresh1, fresh2 = fresh[:size], fresh[size:]
        one = stacked([o[norm, b, 0, 0:1] for o, b in others_of], size)
        two = stacked([o[norm, b, 0, 1:2] for o, b in others_of], size)
        m = (one + fresh1) / count
        v = (two + fresh2) / count - m * m
        inv = lax.rsqrt(v + EPS)
        wide = exact(jnp.concatenate([m, inv], axis=0), member_t)
        return fresh1, fresh2, wide[:size], wide[size:]

    def widened(row, image):
        src = lat_ref[image, 0] if row == 1 else halo[0 if row == 0 else 1, image, 0]
        return src.astype(f32)

    pairs = [(r, b) for r in range(3) for b in range(images)]
    fresh1, fresh2, mean, inv = statistics([widened(r, b) for r, b in pairs], 0, [(others[r], b) for r, b in pairs])
    for b in range(images):
        i = images + b
        sums_out[0, b, 0, 0:1] = fresh1[i : i + 1]
        sums_out[0, b, 0, 1:2] = fresh2[i : i + 1]
    pump(1)
    inside = [jnp.where(me > 0, 1.0, 0.0).astype(f32), None, jnp.where(me < n - 1, 1.0, 0.0).astype(f32)]
    for i, (r, b) in enumerate(pairs):
        u = (widened(r, b) - mean[i : i + 1]) * inv[i : i + 1] * gain_ref[0:1, :]
        u = u / (1.0 + jnp.exp(-u))
        if inside[r] is not None:
            u = u * inside[r]
        act[r, pl.ds(b * columns, columns)] = u.astype(bf16)

    def tap(c):
        acc = None
        for a in (1, 0, 2):
            conv_loads[a][c].wait()
            part = jnp.dot(act[a], conv_w[a, c], preferred_element_type=f32)
            acc = part if acc is None else acc + part
        return acc

    place = lax.broadcasted_iota(jnp.int32, (tokens, channels), 0)
    first_col = place == 0
    last_col = place == columns - 1
    for b in range(1, images):
        first_col = first_col | (place == b * columns)
        last_col = last_col | (place == (b + 1) * columns - 1)
    left = jnp.where(first_col, 0.0, pltpu.roll(tap(0), 1, 0))
    pump(1)
    conv = left + tap(1)
    pump(1)
    conv = conv + jnp.where(last_col, 0.0, pltpu.roll(tap(2), tokens - 1, 0))
    lat = jnp.concatenate([widened(1, b) for b in range(images)], axis=0)
    hidden = (lat + conv + temb).astype(bf16)
    wide_hidden = hidden.astype(f32)
    blocks = [wide_hidden[b * columns : (b + 1) * columns] for b in range(images)]
    fresh1, fresh2, mean, inv = statistics(blocks, 1, [(others[1], b) for b in range(images)])
    normed = []
    for b in range(images):
        sums_out[1, b, 0, 0:1] = fresh1[b : b + 1]
        sums_out[1, b, 0, 1:2] = fresh2[b : b + 1]
        s = ((blocks[b] - mean[b : b + 1]) * inv[b : b + 1] * gain_ref[1:2, :]).astype(bf16)
        states_ref[b, 0] = s
        normed.append(s)
    states = jnp.concatenate(normed, axis=0)
    store_sums = pltpu.make_async_copy(sums_out.at[pl.ds(0, 2)], nsums_ref, small_sem.at[5])
    store_sums.start()
    pump(1)

    for load_ in qkv_loads:
        load_.wait()
    q_s[...] = jnp.dot(states, qkv_w[0], preferred_element_type=f32).astype(bf16)
    for which, dest in ((1, keys), (2, values)):
        made = jnp.dot(states, qkv_w[which], preferred_element_type=f32).astype(bf16)
        for b in range(images):
            dest[b, 0] = made[b * columns : (b + 1) * columns]
    pump(1)
    for image in range(images):
        project_rows(image, 1, 1)

    factor = math.log2(math.e) / math.sqrt(HEAD_DIM)

    def attend(start, size, begin, end):
        pack = 0
        for b in range(images):
            for c0 in range(0, channels, PACK * HEAD_DIM):
                c1 = min(c0 + PACK * HEAD_DIM, channels)
                heads = (c1 - c0) // HEAD_DIM
                rows = heads * columns
                qt = q_s[pl.ds(b * columns, columns), c0:c1]
                lane = lax.broadcasted_iota(jnp.int32, (columns, c1 - c0), 1)
                own = [(lane >= h * HEAD_DIM) & (lane < (h + 1) * HEAD_DIM) for h in range(heads)]

                def mixed(x):
                    out = jnp.where(own[0], x[0:columns], 0.0)
                    for h in range(1, heads):
                        out = jnp.where(own[h], x[h * columns : (h + 1) * columns], out)
                    return out

                qb = jnp.concatenate([jnp.where(own[h], qt, jnp.zeros_like(qt)) for h in range(heads)], axis=0)
                kk = keys[b, pl.ds(start, size), :, c0:c1].reshape(size * columns, c1 - c0)
                vv = values[b, pl.ds(start, size), :, c0:c1].reshape(size * columns, c1 - c0)
                s = lax.dot_general(qb, kk, (((1,), (1,)), ((), ())), preferred_element_type=f32)
                top = jnp.max(s, axis=1, keepdims=True)
                if not begin:
                    before = max_s[pack, pl.ds(0, rows)]
                    top = jnp.maximum(top, before)
                e = jnp.exp2((s - top) * factor)
                den = jnp.sum(e, axis=1, keepdims=True)
                mix = mixed(jnp.dot(e.astype(bf16), vv, preferred_element_type=f32))
                if not begin:
                    scale = jnp.exp2((before - top) * factor)
                    den = den + den_s[pack, pl.ds(0, rows)] * scale
                    mix = mix + mix_s[pl.ds(b * columns, columns), c0:c1] * mixed(scale)
                if end:
                    att_s[pl.ds(b * columns, columns), c0:c1] = (mix / mixed(den)).astype(bf16)
                else:
                    max_s[pack, pl.ds(0, rows)] = top
                    den_s[pack, pl.ds(0, rows)] = den
                    mix_s[pl.ds(b * columns, columns), c0:c1] = mix
                pack += 1

    if last <= 4:
        for step in range(1, last - 1):
            drain(step)
            project(step, 0, pump)
        drain(last - 2)
        cut = 2 + 4 * (last - 2)
        attend(0, cut, True, False)
        drain(last - 1)
    else:
        drain(2)
        project(1, 0)

        @pl.loop(3, last - 1)
        def _(step):
            forward(step, 0)
            project(step - 1, 0)

        forward(last - 1, 1)
        project(last - 2, 0)
        cut = 2 + 4 * (last - 2)
        attend(0, cut, True, False)
    project(last - 1, 1)
    if last <= 4:
        drain(last)
    else:
        forward(last, 2)
    project(last, 2)
    attend(cut, n - cut, False, True)

    out_load.wait()
    result = wide_hidden + jnp.dot(att_s[...], out_w[...], preferred_element_type=f32)
    for b in range(images):
        block_ref[b, 0] = result[b * columns : (b + 1) * columns].astype(bf16)

    store_sums.wait()

    @pl.loop(1, n)
    def _(d):
        sum_copy(d).wait_send()

    @pl.when(me < n - 1)
    def _():
        halo_copy(0).wait_send()

    @pl.when(me > 0)
    def _():
        halo_copy(1).wait_send()

    for image in range(images):
        own_core_copy(image).wait_send()
    for i in range(2 * images):
        ring_copy(1, i, first=True).wait_send()

        @pl.loop(2, last)
        def _(step):
            ring_copy(step, i).wait_send()

        @pl.loop(1, last)
        def _(step):
            core_copy(step, i).wait_send()

    for i in range(images):
        ring_copy(last, i, final=True).wait_send()
        core_copy(last, i, final=True).wait_send()


def settle(block_in, states_in, sums_in, block_ref, states_ref, sums_ref, sem):
    copies = [
        pltpu.make_async_copy(src, dst, sem.at[i])
        for i, (src, dst) in enumerate(((block_in, block_ref), (states_in, states_ref), (sums_in, sums_ref)))
    ]
    for copy in copies:
        copy.start()
    for copy in copies:
        copy.wait()


def solution(mesh):
    n = mesh.shape["patch"]
    width = snake_width(mesh)

    def local(latent, stale_states, stale_sums, timestep, norm_gain, conv_weight, time_weight, qkv_weight, out_weight):
        images, row_count, columns, channels = latent.shape
        assert row_count == 1 and n % 4 == 0 and n >= 8 and images % 2 == 0
        vmem = pl.BlockSpec(memory_space=pltpu.VMEM)
        anywhere = pl.BlockSpec(memory_space=pl.ANY)
        bf16 = jnp.bfloat16
        dma = pltpu.SemaphoreType.DMA
        steps = n // 4 + 1
        packs = images * -(-channels // (PACK * HEAD_DIM))
        made = pl.pallas_call(
            functools.partial(body, n, width),
            out_shape=(
                jax.ShapeDtypeStruct(latent.shape, bf16),
                jax.ShapeDtypeStruct(latent.shape, bf16),
                jax.ShapeDtypeStruct(stale_sums.shape, jnp.float32),
            ),
            in_specs=[anywhere] * 9,
            out_specs=(vmem, vmem, anywhere),
            scratch_shapes=[
                pltpu.SMEM(timestep.shape, jnp.int32),
                pltpu.VMEM(latent.shape, bf16),
                pltpu.VMEM(latent.shape, bf16),
                pltpu.VMEM(norm_gain.shape, jnp.float32),
                pltpu.VMEM(conv_weight.shape, bf16),
                pltpu.VMEM(time_weight.shape, bf16),
                pltpu.VMEM(qkv_weight.shape, bf16),
                pltpu.VMEM(out_weight.shape, bf16),
                pltpu.VMEM((2,) + latent.shape, bf16),
                pltpu.VMEM((n + 1,) + stale_sums.shape, jnp.float32),
                pltpu.VMEM((3,) + stale_sums.shape[1:], jnp.float32),
                pltpu.VMEM((images, n, columns, channels), bf16),
                pltpu.VMEM((images, n, columns, channels), bf16),
                pltpu.VMEM((images, n, columns, channels), bf16),
                pltpu.VMEM((3, images * columns, channels), bf16),
                pltpu.VMEM((images * columns, channels), bf16),
                pltpu.VMEM((images * columns, channels), bf16),
                pltpu.VMEM((packs, PACK * columns, 1), jnp.float32),
                pltpu.VMEM((packs, PACK * columns, 1), jnp.float32),
                pltpu.VMEM((images * columns, channels), jnp.float32),
                dma((14,)),
                dma((6,)),
                dma((steps, 2 * images)),
                dma((steps, 2 * images)),
                dma((steps, 2 * images)),
                dma((steps, 2 * images)),
                dma((2,)),
                dma((2,)),
                dma((n,)),
                dma((n,)),
            ],
            compiler_params=pltpu.CompilerParams(
                collective_id=0, has_side_effects=True, vmem_limit_bytes=60 * 1024 * 1024
            ),
        )(timestep, latent, stale_states, stale_sums, norm_gain, conv_weight, time_weight, qkv_weight, out_weight)
        return pl.pallas_call(
            settle,
            out_shape=tuple(jax.ShapeDtypeStruct(x.shape, x.dtype) for x in made),
            in_specs=[vmem] * 3,
            out_specs=(anywhere,) * 3,
            scratch_shapes=[dma((3,))],
        )(*made)

    in_specs = (
        P("groups", "patch", None, None),
        P("groups", "patch", None, None),
        P(None, "groups", "patch", None, None),
        P("groups"),
        P(),
        P(),
        P(),
        P(),
        P(),
    )
    out_specs = (
        P("groups", "patch", None, None),
        P("groups", "patch", None, None),
        P(None, "groups", "patch", None, None),
    )
    return jax.shard_map(local, mesh=mesh, in_specs=in_specs, out_specs=out_specs, check_vma=False)
```

time: 38.3 us -> 35.2 us (0.919)
  Pallas kernels: 36.8 us -> 33.8 us
    pallas_call x1, Pallas kernels: 35.1 us -> 32 us  [local(): pl.pallas_call(functools.partial(body, n, width), out_shape=(jax.ShapeDty...]
where the time goes in v1:
time: 35.2 us; the launch traced here: 35.1 us
  Pallas kernels  33.8 us (96%)
  between operations  1.29 us (4%)
    pallas_call x1, Pallas kernels, local(): pl.pallas_call(functools.partial(body, n, width), out_shape=(jax.ShapeDty...  32 us
    pallas_call x1, Pallas kernels, local(): pl.pallas_call(settle, out_shape=tuple((jax.ShapeDtypeStruct(x.shape, x.d...  1.74 us

profile of v1, /device:TPU:1, one launch (start us, length us, event | category | flops | bytes accessed | tf_op | source)
XLA Modules:
  0.0 35.1 jit_solution(7416085415096009334)
XLA Ops:
  1.3 32.0 %shard_map.112 = (bf16[2,1,64,640]{3,2,1,0:T(8,128)(2,1)}, bf16[2,1,64,640]{3,2,1,0:T(8,128)(2,1)}, f32[2,2,1,2,16]{4,3,2,1,0:T(2,128)}) custom-call(s32[1]{0:T(128)S(6)} %copy.12.t_hbm, bf16[2,1,64,640]{3,2,1,0:T(8,128)(2,1)} %lat_hbm.1, bf16[2,1,64,640]{3,2,1,0:T(8,128)(2,1)} %stale_hbm.1, f32[2,2,1,2,16]{4,3,2,1,0:T(2,128)} %ssum_hbm.1, ...), custom_call_target="tpu_custom_call" | custom-call | tf_op jit(solution)/shard_map/pallas_call | solution.py:476
  33.3 1.7 %shard_map.113 = (bf16[2,1,64,640]{3,2,1,0:T(8,128)(2,1)}, bf16[2,1,64,640]{3,2,1,0:T(8,128)(2,1)}, f32[2,2,1,2,16]{4,3,2,1,0:T(2,128)}) custom-call(bf16[2,1,64,640]{3,2,1,0:T(8,128)(2,1)} %get-tuple-element.6.block_in, bf16[2,1,64,640]{3,2,1,0:T(8,128)(2,1)} %get-tuple-element.7.states_in, f32[2,2,1,2,16]{4,3,2,1,0:T(2,128)} %get-tuple-element.8.sums_in), custom_call_target="tpu_custom_call" | custom-call | tf_op jit(solution)/shard_map/pallas_call | solution.py:521

commit v2 on v1

v2 whole, which is shorter than its diff:
```python
import functools
import math

import jax
import jax.numpy as jnp
from jax import lax
from jax.experimental import pallas as pl
from jax.experimental.pallas import tpu as pltpu
from jax.sharding import PartitionSpec as P

HEAD_DIM = 64
PACK = 4
EPS = 1e-05
PUMPS = (1, 1, 1, 1, 0, 1, 1, 1)


def snake_width(mesh):
    try:
        axis = mesh.axis_names.index("patch")
        line = mesh.devices
        for other in range(line.ndim - 1, -1, -1):
            if other != axis:
                line = line.take(0, axis=other)
        rows = {tuple(d.coords)[1] for d in line.flat}
        return 2 if len(rows) == 2 and tuple(line.flat[2].coords)[1] != tuple(line.flat[0].coords)[1] else 1
    except Exception:
        return 1


def ring_pos(chip, chips, width):
    if width == 1:
        return chip
    long = chips // 2
    z, y = chip // 2, chip % 2
    return z * (1 - y) + (2 * long - 1 - z) * y


def ring_chip(pos, chips, width):
    if width == 1:
        return pos
    long = chips // 2
    y = pos // long
    z = pos * (1 - y) + (2 * long - 1 - pos) * y
    return z * 2 + y


def body(n, width, t_hbm, lat_hbm, stale_hbm, ssum_hbm, gain_hbm, conv_hbm, time_hbm, qkv_hbm, out_hbm,
         block_ref, states_ref, nsums_ref,
         t_ref, lat_ref, stale_ref, gain_ref, conv_w, time_w, qkv_w, out_w, halo, sums_all, sums_out, rx, keys, values,
         act, q_s, flip_w, max_s, den_s, mix_s, block_s, states_s,
         w_sem, small_sem, ring_send, ring_recv, core_send, core_recv, halo_send, halo_recv, sum_send, sum_recv, known):
    images, _, columns, channels = lat_ref.shape
    groups = ssum_hbm.shape[-1]
    f32, bf16 = jnp.float32, jnp.bfloat16
    tokens = images * columns
    chips, last = n // 2, n // 4
    count = float(n * columns * (channels // groups))
    me = lax.axis_index("patch")
    core = me % 2
    pos = ring_pos(me // 2, chips, width)
    ahead = ring_chip((pos + 1) % chips, chips, width) * 2
    behind = ring_chip((pos + chips - 1) % chips, chips, width) * 2
    target = ahead * (1 - core) + behind * core + core
    sibling = me + 1 - 2 * core
    source = ahead * core + behind * (1 - core) + core
    late = me >= n // 2
    MESH = pl.DeviceIdType.MESH

    barrier = pltpu.get_barrier_semaphore()

    def greet(semaphore, where):
        pl.semaphore_signal(semaphore, inc=1, device_id={"patch": where}, device_id_type=MESH)

    greet(barrier, source)
    greet(barrier, sibling)

    def load(src, dst, index):
        return pltpu.make_async_copy(src, dst, w_sem.at[index])

    conv_loads = [
        [load(conv_hbm.at[a, c], conv_w.at[a, :, pl.ds(c * channels, channels)], 3 * a + c) for c in range(3)]
        for a in range(3)
    ]
    time_load = load(time_hbm, time_w, 9)
    qkv_loads = [load(qkv_hbm.at[i], qkv_w.at[i], 10 + i) for i in range(3)]
    out_load = load(out_hbm, out_w, 13)
    small = [
        pltpu.make_async_copy(src, dst, small_sem.at[i])
        for i, (src, dst) in enumerate(
            ((stale_hbm, stale_ref), (ssum_hbm, sums_all.at[0]), (lat_hbm, lat_ref), (t_hbm, t_ref), (gain_hbm, gain_ref))
        )
    ]
    for copy in small:
        copy.start()
    def remote(src, dst, send, recv, where):
        return pltpu.make_async_remote_copy(src_ref=src, dst_ref=dst, send_sem=send, recv_sem=recv,
                                            device_id={"patch": where}, device_id_type=MESH)

    def sum_copy(d):
        return remote(sums_all.at[0], sums_all.at[d], sum_send.at[d], sum_recv.at[d], (me + d) % n)

    def halo_copy(slot):
        where = (me + 1) % n if slot == 0 else (me + n - 1) % n
        return remote(lat_ref, halo.at[slot], halo_send.at[slot], halo_recv.at[slot], where)

    def slot_of(step, direction, row, final):
        return 2 + 4 * (step - 1) + row + (0 if final else 2 * direction)

    def chunk(i, direction):
        return (direction if i < images else 1 - direction), i % images

    def ring_copy(step, i, first=False, final=False):
        row, image = chunk(i, core)
        if first:
            src = stale_ref.at[image, 0] if i < images else rx.at[image, 1]
        else:
            src = rx.at[image, slot_of(step - 1, core, row, False)]
        return remote(src, rx.at[image, slot_of(step, core, row, final)],
                      ring_send.at[step, i], ring_recv.at[step, i], target)

    def core_copy(step, i, final, direction=None):
        direction = core if direction is None else direction
        row, image = chunk(i, direction)
        ref = rx.at[image, slot_of(step, direction, row, final)]
        return remote(ref, ref, core_send.at[step, i], core_recv.at[step, i], sibling)

    def share_copies(step, direction=None):
        direction = core if direction is None else direction
        start = slot_of(step, direction, 0, False)
        begin = pl.multiple_of(start * columns, 2 * columns)
        refs = [keys.at[b, pl.ds(start, 2)] for b in range(images)]
        refs += [values.at[b, :, pl.ds(begin, 2 * columns)] for b in range(images)]
        return [
            remote(ref, ref, core_send.at[step, i], core_recv.at[step, i], sibling) for i, ref in enumerate(refs)
        ]

    def share(step):
        for copy in share_copies(step):
            copy.start()

    def own_core_copy(image):
        return remote(stale_ref.at[image, 0], rx.at[image, 1], core_send.at[0, image],
                      core_recv.at[0, image], sibling)

    for copy in small:
        copy.wait()
    time_load.start()
    qkv_loads[2].start()
    qkv_loads[1].start()
    for a in (1, 0, 2):
        for c in range(3):
            conv_loads[a][c].start()
    qkv_loads[0].start()
    out_load.start()
    pl.semaphore_wait(barrier, 2)

    greet(known.at[0], target)
    for image in range(images):
        own_core_copy(image).start()
    for image in range(images):
        ring_copy(1, image, first=True).start()

    @pl.when(core == 0)
    def _():
        halo_copy(0).start()

    @pl.when(core == 1)
    def _():
        halo_copy(1).start()

    def heard(spread):
        pl.semaphore_wait(known.at[spread], 1)
        if not isinstance(spread, int) or spread < last - 1:
            greet(known.at[spread + 1], target)

    @pl.loop(0, last - 2)
    def _(spread):
        heard(spread)

    for image in range(images):
        own_core_copy(image).wait_recv()
        ring_copy(1, images + image, first=True).start()

    def event(step, i, kind):
        ring_copy(step, i, first=True, final=kind == 2).wait_recv()
        if kind == 0 or (kind == 1 and i < images):
            ring_copy(step + 1, i, final=kind == 1).start()
        if kind:
            core_copy(step, i, kind == 2).start()

    def count_of(kind):
        return images if kind == 2 else 2 * images

    def kind_of(step):
        return 2 if step == last else 1 if step == last - 1 else 0

    static = [s for s in range(1, last + 1) if last <= 4 or s <= 2]
    queue = [(s, i, kind_of(s)) for s in static for i in range(count_of(kind_of(s)))]

    def pump(amount=1):
        for _ in range(min(amount, len(queue))):
            event(*queue.pop(0))

    def drain(step):
        while queue and queue[0][0] <= step:
            pump()

    def forward(step, kind):
        for i in range(count_of(kind)):
            event(step, i, kind)

    @pl.when(me == 0)
    def _():
        halo[0] = jnp.zeros_like(lat_ref)

    @pl.when(me == n - 1)
    def _():
        halo[1] = jnp.zeros_like(lat_ref)

    across = (((1,), (1,)), ((), ()))

    def project_made(pieces):
        rows = jnp.concatenate([piece[2] for piece in pieces], axis=0)
        made = jnp.dot(rows, qkv_w[1], preferred_element_type=f32).astype(bf16)
        turned = lax.dot_general(flip_w[...], rows, across, preferred_element_type=f32).astype(bf16)
        span = 2 * columns
        for i, (image, start, _) in enumerate(pieces):
            at = slice(i * span, (i + 1) * span)
            begin = start * columns
            if not isinstance(begin, int):
                begin = pl.multiple_of(begin, span)
            keys[image, pl.ds(start, 2)] = made[at].reshape(2, columns, channels)
            values[image, :, pl.ds(begin, span)] = turned[:, at]

    def held(image, start):
        return image, start, rx[image, pl.ds(start, 2)].reshape(2 * columns, channels)

    def project(*steps):
        project_made([held(b, slot_of(step, core, 0, False)) for step in steps for b in range(images)])

    def arrived(step):
        for copy in share_copies(step, 1 - core):
            copy.wait_recv()

    def project_raw(step, final):
        for i in range(images if final else 2 * images):
            core_copy(step, i, final, direction=1 - core).wait_recv()
        first = slot_of(step, 0, 0, final)
        starts = [first] if final else [first, first + 2]
        project_made([held(b, start) for b in range(images) for start in starts])

    ch = lax.broadcasted_iota(jnp.int32, (channels, groups), 0)
    gr = lax.broadcasted_iota(jnp.int32, (channels, groups), 1) * (channels // groups)
    member = jnp.where((ch >= gr) & (ch < gr + channels // groups), 1.0, 0.0).astype(bf16)
    ch_t = lax.broadcasted_iota(jnp.int32, (groups, channels), 1)
    gr_t = lax.broadcasted_iota(jnp.int32, (groups, channels), 0) * (channels // groups)
    member_t = jnp.where((ch_t >= gr_t) & (ch_t < gr_t + channels // groups), 1.0, 0.0).astype(bf16)

    def exact(x, picks):
        rows = x.shape[0]
        hi = x.astype(bf16)
        rest = x - hi.astype(f32)
        mid = rest.astype(bf16)
        lo = (rest - mid.astype(f32)).astype(bf16)
        y = jnp.dot(jnp.concatenate([hi, mid, lo], axis=0), picks, preferred_element_type=f32)
        return y[2 * rows :] + y[rows : 2 * rows] + y[:rows]

    firsts = [queue.pop(0) for _ in range(3)]

    @pl.when(jnp.logical_not(late))
    def _():
        event(*firsts[0])

    heard(last - 2)

    @pl.when(jnp.logical_not(late))
    def _():
        event(*firsts[1])
        event(*firsts[2])

    heard(last - 1)
    greet(known.at[last], sibling)
    pl.semaphore_wait(known.at[last], 1)

    @pl.loop(1, n)
    def _(d):
        sum_copy(d).start()

    @pl.when((core == 1) & (me < n - 1))
    def _():
        halo_copy(0).start()

    @pl.when((core == 0) & (me > 0))
    def _():
        halo_copy(1).start()

    @pl.when(late)
    def _():
        for first in firsts:
            event(*first)

    freq_count = time_w.shape[0] // 2
    idx = lax.broadcasted_iota(jnp.int32, (8, 2 * freq_count), 1)
    low = idx < freq_count
    freqs = jnp.exp(-math.log(10000.0) * jnp.where(low, idx, idx - freq_count).astype(f32) / freq_count)
    angles = t_ref[...].astype(f32) * freqs
    emb = jnp.where(low, jnp.cos(angles), jnp.sin(angles))
    emb = emb / (1.0 + jnp.exp(-emb))
    time_load.wait()
    temb = exact(emb, time_w[...])[0:1]

    qkv_loads[2].wait()
    diagonal = lax.broadcasted_iota(jnp.int32, (channels, channels), 0) == lax.broadcasted_iota(
        jnp.int32, (channels, channels), 1
    )
    unit = jnp.where(diagonal, 1.0, 0.0).astype(bf16)
    flip_w[...] = lax.dot_general(unit, qkv_w[2], across, preferred_element_type=f32).astype(bf16)

    drain(1)
    qkv_loads[1].wait()
    project(1)
    pump(PUMPS[0])
    share(1)

    @pl.loop(1, n)
    def _(d):
        sum_copy(d).wait_recv()

    total = sums_all[0]
    total = lax.fori_loop(1, n, lambda d, acc: acc + sums_all[d], total)
    others = [total - sums_all[1], total - sums_all[0], total - sums_all[n - 1]]

    @pl.when(me > 0)
    def _():
        halo_copy(0).wait_recv()

    @pl.when(me < n - 1)
    def _():
        halo_copy(1).wait_recv()

    pump(PUMPS[1])

    def stacked(rows, size):
        pad = size - len(rows)
        if pad:
            rows = rows + [jnp.zeros((pad, rows[0].shape[1]), f32)]
        return jnp.concatenate(rows, axis=0)

    def statistics(blocks, norm, others_of):
        size = -(-len(blocks) // 8) * 8
        firsts = stacked([jnp.sum(x, axis=0, keepdims=True) for x in blocks], size)
        seconds = stacked([jnp.sum(x * x, axis=0, keepdims=True) for x in blocks], size)
        fresh = exact(jnp.concatenate([firsts, seconds], axis=0), member)
        fresh1, fresh2 = fresh[:size], fresh[size:]
        one = stacked([o[norm, b, 0, 0:1] for o, b in others_of], size)
        two = stacked([o[norm, b, 0, 1:2] for o, b in others_of], size)
        m = (one + fresh1) / count
        v = (two + fresh2) / count - m * m
        inv = lax.rsqrt(v + EPS)
        wide = exact(jnp.concatenate([m, inv], axis=0), member_t)
        return fresh1, fresh2, wide[:size], wide[size:]

    def widened(row, image):
        src = lat_ref[image, 0] if row == 1 else halo[0 if row == 0 else 1, image, 0]
        return src.astype(f32)

    pairs = [(r, b) for r in range(3) for b in range(images)]
    fresh1, fresh2, mean, inv = statistics([widened(r, b) for r, b in pairs], 0, [(others[r], b) for r, b in pairs])
    for b in range(images):
        i = images + b
        sums_out[0, b, 0, 0:1] = fresh1[i : i + 1]
        sums_out[0, b, 0, 1:2] = fresh2[i : i + 1]
    pump(PUMPS[2])
    inside = [jnp.where(me > 0, 1.0, 0.0).astype(f32), None, jnp.where(me < n - 1, 1.0, 0.0).astype(f32)]
    for i, (r, b) in enumerate(pairs):
        u = (widened(r, b) - mean[i : i + 1]) * inv[i : i + 1] * gain_ref[0:1, :]
        u = u / (1.0 + jnp.exp(-u))
        if inside[r] is not None:
            u = u * inside[r]
        act[r, pl.ds(b * columns, columns)] = u.astype(bf16)

    taps = None
    for a in (1, 0, 2):
        for c in range(3):
            conv_loads[a][c].wait()
        part = jnp.dot(act[a], conv_w[a], preferred_element_type=f32)
        taps = part if taps is None else taps + part
    taps = [taps[:, c * channels : (c + 1) * channels] for c in range(3)]

    place = lax.broadcasted_iota(jnp.int32, (tokens, channels), 0)
    first_col = place == 0
    last_col = place == columns - 1
    for b in range(1, images):
        first_col = first_col | (place == b * columns)
        last_col = last_col | (place == (b + 1) * columns - 1)
    conv = jnp.where(first_col, 0.0, pltpu.roll(taps[0], 1, 0)) + taps[1]
    conv = conv + jnp.where(last_col, 0.0, pltpu.roll(taps[2], tokens - 1, 0))
    pump(PUMPS[3])
    if last <= 4:
        for step in range(2, last - 1):
            drain(step)
            project(step)
            share(step)
    lat = jnp.concatenate([widened(1, b) for b in range(images)], axis=0)
    hidden = (lat + conv + temb).astype(bf16)
    wide_hidden = hidden.astype(f32)
    blocks = [wide_hidden[b * columns : (b + 1) * columns] for b in range(images)]
    fresh1, fresh2, mean, inv = statistics(blocks, 1, [(others[1], b) for b in range(images)])
    normed = []
    for b in range(images):
        sums_out[1, b, 0, 0:1] = fresh1[b : b + 1]
        sums_out[1, b, 0, 1:2] = fresh2[b : b + 1]
        s = ((blocks[b] - mean[b : b + 1]) * inv[b : b + 1] * gain_ref[1:2, :]).astype(bf16)
        states_s[b, 0] = s
        normed.append(s)
    states = jnp.concatenate(normed, axis=0)
    store_sums = pltpu.make_async_copy(sums_out.at[pl.ds(0, 2)], nsums_ref, small_sem.at[5])
    store_sums.start()
    store_states = pltpu.make_async_copy(states_s, states_ref, small_sem.at[6])
    store_states.start()
    pump(PUMPS[5])

    qkv_loads[0].wait()
    q_s[...] = jnp.dot(states, qkv_w[0], preferred_element_type=f32).astype(bf16)
    project_made([(b, 0, jnp.concatenate([normed[b], rx[b, 1]], axis=0)) for b in range(images)])
    pump(PUMPS[6])

    factor = math.log2(math.e) / math.sqrt(HEAD_DIM)

    pair = 2 * columns

    def sent():
        store_sums.wait()
        store_states.wait()

        @pl.loop(1, n)
        def _(d):
            sum_copy(d).wait_send()

        @pl.when(me < n - 1)
        def _():
            halo_copy(0).wait_send()

        @pl.when(me > 0)
        def _():
            halo_copy(1).wait_send()

        for image in range(images):
            own_core_copy(image).wait_send()
        for i in range(2 * images):
            ring_copy(1, i, first=True).wait_send()

            @pl.loop(2, last)
            def _(step):
                ring_copy(step, i).wait_send()

        @pl.loop(1, last - 1)
        def _(step):
            for copy in share_copies(step):
                copy.wait_send()

    def attend(start, size, begin, end):
        spans = [
            (b, c0, min(c0 + PACK * HEAD_DIM, channels))
            for b in range(images)
            for c0 in range(0, channels, PACK * HEAD_DIM)
        ]

        def score(b, c0, c1):
            heads = (c1 - c0) // HEAD_DIM
            qt = q_s[pl.ds(b * columns, columns), c0:c1]
            lane = lax.broadcasted_iota(jnp.int32, (columns, c1 - c0), 1)
            own = [(lane >= h * HEAD_DIM) & (lane < (h + 1) * HEAD_DIM) for h in range(heads)]
            qb = jnp.concatenate([jnp.where(own[h], qt, jnp.zeros_like(qt)) for h in range(heads)], axis=0)
            kk = keys[b, pl.ds(start, size), :, c0:c1].reshape(size * columns, c1 - c0)
            return lax.dot_general(kk, qb, across, preferred_element_type=f32)

        blocks_of = [[] for _ in range(images)]
        ahead_s = score(*spans[0])
        for pack, (b, c0, c1) in enumerate(spans):
            heads = (c1 - c0) // HEAD_DIM
            rows = heads * columns
            s = ahead_s
            if pack + 1 < len(spans):
                ahead_s = score(*spans[pack + 1])
            vv = values[b, c0:c1, pl.ds(start * columns, size * columns)]
            top = jnp.max(s, axis=0, keepdims=True)
            if not begin:
                before = max_s[pack, :, pl.ds(0, rows)]
                top = jnp.maximum(top, before)
            e = jnp.exp2((s - top) * factor)
            den = jnp.sum(e, axis=0, keepdims=True)
            if not begin:
                scale = jnp.exp2((before - top) * factor)
                den = den + den_s[pack, :, pl.ds(0, rows)] * scale
            o = jnp.dot(vv, e.astype(bf16), preferred_element_type=f32)
            if not end:
                max_s[pack, :, pl.ds(0, rows)] = top
                den_s[pack, :, pl.ds(0, rows)] = den
            for h in range(heads):
                j = h // 2 * pair
                at = pl.ds(c0 + h * HEAD_DIM, HEAD_DIM)
                part = o[h * HEAD_DIM : (h + 1) * HEAD_DIM, j : j + pair]
                if not begin:
                    part = part + mix_s[b, at] * scale[:, j : j + pair]
                if not end:
                    mix_s[b, at] = part
                else:
                    part = part / den[:, j : j + pair]
                    blocks_of[b].append(part if h % 2 == b % 2 else pltpu.roll(part, columns, 1))
        if end:
            lane = lax.broadcasted_iota(jnp.int32, (HEAD_DIM, pair), 1)
            merged = [jnp.where(lane < columns, x, y) for x, y in zip(*blocks_of)]
            return jnp.concatenate(merged, axis=0).astype(bf16)

    if last > 4:
        drain(2)

        @pl.loop(3, last - 1)
        def _(step):
            forward(step, 0)
            project(step - 1)
            share(step - 1)

        project(last - 2)
        share(last - 2)

    @pl.loop(1, last - 1)
    def _(step):
        arrived(step)

    cut = slot_of(last - 1, 0, 0, False)
    if last <= 4:
        pump(PUMPS[7])
    attend(0, cut, True, False)
    sent()
    if last <= 4:
        drain(last - 1)
    else:
        forward(last - 1, 1)
    project_raw(last - 1, False)
    if last <= 4:
        drain(last)
    else:
        forward(last, 2)
    project_raw(last, True)
    attended = attend(cut, n - cut, False, True)

    out_load.wait()
    result = wide_hidden + lax.dot_general(
        attended, out_w[...], (((0,), (0,)), ((), ())), preferred_element_type=f32
    )
    for b in range(images):
        block_s[b, 0] = result[b * columns : (b + 1) * columns].astype(bf16)
    store_block = pltpu.make_async_copy(block_s, block_ref, small_sem.at[7])
    store_block.start()
    for i in range(2 * images):
        core_copy(last - 1, i, False).wait_send()
    for i in range(images):
        ring_copy(last, i, final=True).wait_send()
        core_copy(last, i, True).wait_send()
    store_block.wait()


def settle(block_in, states_in, sums_in, block_ref, states_ref, sums_ref, sem):
    copies = [
        pltpu.make_async_copy(src, dst, sem.at[i])
        for i, (src, dst) in enumerate(((block_in, block_ref), (states_in, states_ref), (sums_in, sums_ref)))
    ]
    for copy in copies:
        copy.start()
    for copy in copies:
        copy.wait()


def solution(mesh):
    n = mesh.shape["patch"]
    width = snake_width(mesh)

    def local(latent, stale_states, stale_sums, timestep, norm_gain, conv_weight, time_weight, qkv_weight, out_weight):
        images, row_count, columns, channels = latent.shape
        assert row_count == 1 and n % 4 == 0 and n >= 8 and images == 2 and columns == HEAD_DIM
        vmem = pl.BlockSpec(memory_space=pltpu.VMEM)
        anywhere = pl.BlockSpec(memory_space=pl.ANY)
        bf16 = jnp.bfloat16
        dma = pltpu.SemaphoreType.DMA
        steps = n // 4 + 1
        packs = images * -(-channels // (PACK * HEAD_DIM))
        made = pl.pallas_call(
            functools.partial(body, n, width),
            out_shape=(
                jax.ShapeDtypeStruct(latent.shape, bf16),
                jax.ShapeDtypeStruct(latent.shape, bf16),
                jax.ShapeDtypeStruct(stale_sums.shape, jnp.float32),
            ),
            in_specs=[pl.BlockSpec(memory_space=pltpu.HBM)] * 9,
            out_specs=(pl.BlockSpec(memory_space=pltpu.HBM),) * 3,
            scratch_shapes=[
                pltpu.VMEM((1, 1), jnp.int32),
                pltpu.VMEM(latent.shape, bf16),
                pltpu.VMEM(latent.shape, bf16),
                pltpu.VMEM(norm_gain.shape, jnp.float32),
                pltpu.VMEM((3, channels, 3 * channels), bf16),
                pltpu.VMEM(time_weight.shape, bf16),
                pltpu.VMEM(qkv_weight.shape, bf16),
                pltpu.VMEM(out_weight.shape, bf16),
                pltpu.VMEM((2,) + latent.shape, bf16),
                pltpu.VMEM((n + 1,) + stale_sums.shape, jnp.float32),
                pltpu.VMEM((3,) + stale_sums.shape[1:], jnp.float32),
                pltpu.VMEM((images, n, columns, channels), bf16),
                pltpu.VMEM((images, n, columns, channels), bf16),
                pltpu.VMEM((images, channels, n * columns), bf16),
                pltpu.VMEM((3, images * columns, channels), bf16),
                pltpu.VMEM((images * columns, channels), bf16),
                pltpu.VMEM((channels, channels), bf16),
                pltpu.VMEM((packs, 1, PACK * columns), jnp.float32),
                pltpu.VMEM((packs, 1, PACK * columns), jnp.float32),
                pltpu.VMEM((images, channels, 2 * columns), jnp.float32),
                pltpu.VMEM(latent.shape, bf16),
                pltpu.VMEM(latent.shape, bf16),
                dma((14,)),
                dma((8,)),
                dma((steps, 2 * images)),
                dma((steps, 2 * images)),
                dma((steps, 2 * images)),
                dma((steps, 2 * images)),
                dma((2,)),
                dma((2,)),
                dma((n,)),
                dma((n,)),
                pltpu.SemaphoreType.REGULAR((n // 4 + 1,)),
            ],
            compiler_params=pltpu.CompilerParams(
                collective_id=0, has_side_effects=True, vmem_limit_bytes=60 * 1024 * 1024
            ),
        )(timestep.reshape(1, 1), latent, stale_states, stale_sums, norm_gain, conv_weight, time_weight, qkv_weight, out_weight)
        return pl.pallas_call(
            settle,
            out_shape=tuple(jax.ShapeDtypeStruct(x.shape, x.dtype) for x in made),
            in_specs=[vmem] * 3,
            out_specs=(anywhere,) * 3,
            scratch_shapes=[dma((3,))],
        )(*made)

    in_specs = (
        P("groups", "patch", None, None),
        P("groups", "patch", None, None),
        P(None, "groups", "patch", None, None),
        P("groups"),
        P(),
        P(),
        P(),
        P(),
        P(),
    )
    out_specs = (
        P("groups", "patch", None, None),
        P("groups", "patch", None, None),
        P(None, "groups", "patch", None, None),
    )
    return jax.shard_map(local, mesh=mesh, in_specs=in_specs, out_specs=out_specs, check_vma=False)
```

time: 35.2 us -> 34.1 us (0.969); the launches traced: 35.1 us -> 33.6 us
  Pallas kernels: 33.8 us -> 32.3 us
    pallas_call x1, Pallas kernels: 32 us -> 30.5 us  [local(): pl.pallas_call(functools.partial(body, n, width), out_shape=(jax.ShapeDty...]
where the time goes in v2:
time: 34.1 us; the launch traced here: 33.6 us
  Pallas kernels  32.3 us (95%)
  between operations  1.29 us (4%)
    pallas_call x1, Pallas kernels, local(): pl.pallas_call(functools.partial(body, n, width), out_shape=(jax.ShapeDty...  30.5 us
    pallas_call x1, Pallas kernels, local(): pl.pallas_call(settle, out_shape=tuple((jax.ShapeDtypeStruct(x.shape, x.d...  1.74 us

profile of v2, /device:TPU:1, one launch (start us, length us, event | category | flops | bytes accessed | tf_op | source)
XLA Modules:
  0.0 33.6 jit_solution(683551580615392071)
XLA Ops:
  1.3 30.5 %shard_map.112 = (bf16[2,1,64,640]{3,2,1,0:T(8,128)(2,1)}, bf16[2,1,64,640]{3,2,1,0:T(8,128)(2,1)}, f32[2,2,1,2,16]{4,3,2,1,0:T(2,128)}) custom-call(s32[1,1]{1,0:T(1,128)} %bitcast.1.t_hbm, bf16[2,1,64,640]{3,2,1,0:T(8,128)(2,1)} %lat_hbm.1, bf16[2,1,64,640]{3,2,1,0:T(8,128)(2,1)} %stale_hbm.1, f32[2,2,1,2,16]{4,3,2,1,0:T(2,128)} %ssum_hbm.1, ...), custom_call_target="tpu_custom_call" | custom-call | tf_op jit(solution)/shard_map/pallas_call | solution.py:589
  31.8 1.7 %shard_map.113 = (bf16[2,1,64,640]{3,2,1,0:T(8,128)(2,1)}, bf16[2,1,64,640]{3,2,1,0:T(8,128)(2,1)}, f32[2,2,1,2,16]{4,3,2,1,0:T(2,128)}) custom-call(bf16[2,1,64,640]{3,2,1,0:T(8,128)(2,1)} %get-tuple-element.6.block_in, bf16[2,1,64,640]{3,2,1,0:T(8,128)(2,1)} %get-tuple-element.7.states_in, f32[2,2,1,2,16]{4,3,2,1,0:T(2,128)} %get-tuple-element.8.sums_in), custom_call_target="tpu_custom_call" | custom-call | tf_op jit(solution)/shard_map/pallas_call | solution.py:637

commit v3 on v2

--- a/solution.py
+++ b/solution.py
@@ -12,6 +12,7 @@
 PACK = 4
 EPS = 1e-05
 PUMPS = (1, 1, 1, 1, 0, 1, 1, 1)
+BETWEEN = (3,)
 
 
 def snake_width(mesh):
@@ -173,13 +174,18 @@
         if not isinstance(spread, int) or spread < last - 1:
             greet(known.at[spread + 1], target)
 
-    @pl.loop(0, last - 2)
-    def _(spread):
-        heard(spread)
+    def heard_first():
+        @pl.loop(0, last - 2)
+        def _(spread):
+            heard(spread)
+
+    pl.when(late)(heard_first)
 
     for image in range(images):
         own_core_copy(image).wait_recv()
         ring_copy(1, images + image, first=True).start()
+
+    pl.when(jnp.logical_not(late))(heard_first)
 
     def event(step, i, kind):
         ring_copy(step, i, first=True, final=kind == 2).wait_recv()
@@ -459,7 +465,7 @@
             for copy in share_copies(step):
                 copy.wait_send()
 
-    def attend(start, size, begin, end):
+    def attend(start, size, begin, end, between=()):
         spans = [
             (b, c0, min(c0 + PACK * HEAD_DIM, channels))
             for b in range(images)
@@ -483,6 +489,8 @@
             s = ahead_s
             if pack + 1 < len(spans):
                 ahead_s = score(*spans[pack + 1])
+            if pack in between:
+                pump()
             vv = values[b, c0:c1, pl.ds(start * columns, size * columns)]
             top = jnp.max(s, axis=0, keepdims=True)
             if not begin:
@@ -532,17 +540,16 @@
     cut = slot_of(last - 1, 0, 0, False)
     if last <= 4:
         pump(PUMPS[7])
-    attend(0, cut, True, False)
+    attend(0, cut, True, False, BETWEEN)
     sent()
     if last <= 4:
         drain(last - 1)
     else:
         forward(last - 1, 1)
-    project_raw(last - 1, False)
+        forward(last, 2)
     if last <= 4:
         drain(last)
-    else:
-        forward(last, 2)
+    project_raw(last - 1, False)
     project_raw(last, True)
     attended = attend(cut, n - cut, False, True)
 

time: 34.1 us -> 32.5 us (0.953); the launches traced: 33.6 us -> 32.4 us
  Pallas kernels: 32.3 us -> 31.1 us
    pallas_call x1, Pallas kernels: 30.5 us -> 29.3 us  [local(): pl.pallas_call(functools.partial(body, n, width), out_shape=(jax.ShapeDty...]
where the time goes in v3:
time: 32.5 us; the launch traced here: 32.4 us
  Pallas kernels  31.1 us (96%)
  between operations  1.29 us (4%)
    pallas_call x1, Pallas kernels, local(): pl.pallas_call(functools.partial(body, n, width), out_shape=(jax.ShapeDty...  29.3 us
    pallas_call x1, Pallas kernels, local(): pl.pallas_call(settle, out_shape=tuple((jax.ShapeDtypeStruct(x.shape, x.d...  1.74 us

profile of v3, /device:TPU:1, one launch (start us, length us, event | category | flops | bytes accessed | tf_op | source)
XLA Modules:
  0.0 32.4 jit_solution(17454681560980695994)
XLA Ops:
  1.3 29.3 %shard_map.112 = (bf16[2,1,64,640]{3,2,1,0:T(8,128)(2,1)}, bf16[2,1,64,640]{3,2,1,0:T(8,128)(2,1)}, f32[2,2,1,2,16]{4,3,2,1,0:T(2,128)}) custom-call(s32[1,1]{1,0:T(1,128)} %bitcast.1.t_hbm, bf16[2,1,64,640]{3,2,1,0:T(8,128)(2,1)} %lat_hbm.1, bf16[2,1,64,640]{3,2,1,0:T(8,128)(2,1)} %stale_hbm.1, f32[2,2,1,2,16]{4,3,2,1,0:T(2,128)} %ssum_hbm.1, ...), custom_call_target="tpu_custom_call" | custom-call | tf_op jit(solution)/shard_map/pallas_call | solution.py:596
  30.6 1.7 %shard_map.113 = (bf16[2,1,64,640]{3,2,1,0:T(8,128)(2,1)}, bf16[2,1,64,640]{3,2,1,0:T(8,128)(2,1)}, f32[2,2,1,2,16]{4,3,2,1,0:T(2,128)}) custom-call(bf16[2,1,64,640]{3,2,1,0:T(8,128)(2,1)} %get-tuple-element.6.block_in, bf16[2,1,64,640]{3,2,1,0:T(8,128)(2,1)} %get-tuple-element.7.states_in, f32[2,2,1,2,16]{4,3,2,1,0:T(2,128)} %get-tuple-element.8.sums_in), custom_call_target="tpu_custom_call" | custom-call | tf_op jit(solution)/shard_map/pallas_call | solution.py:644

commit v4 on v3

--- a/solution.py
+++ b/solution.py
@@ -11,7 +11,7 @@
 HEAD_DIM = 64
 PACK = 4
 EPS = 1e-05
-PUMPS = (1, 1, 1, 1, 0, 1, 1, 1)
+PUMPS = (2, 1, 1, 1, 0, 1, 1, 1)
 BETWEEN = (3,)
 
 

time: 32.5 us -> 31.8 us (0.978)
  Pallas kernels: 31.1 us -> 30.1 us
    pallas_call x1, Pallas kernels: 29.3 us -> 28.4 us  [local(): pl.pallas_call(functools.partial(body, n, width), out_shape=(jax.ShapeDty...]
where the time goes in v4:
time: 31.8 us; the launch traced here: 31.4 us
  Pallas kernels  30.1 us (95%)
  between operations  1.29 us (4%)
    pallas_call x1, Pallas kernels, local(): pl.pallas_call(functools.partial(body, n, width), out_shape=(jax.ShapeDty...  28.4 us
    pallas_call x1, Pallas kernels, local(): pl.pallas_call(settle, out_shape=tuple((jax.ShapeDtypeStruct(x.shape, x.d...  1.74 us

profile of v4, /device:TPU:1, one launch (start us, length us, event | category | flops | bytes accessed | tf_op | source)
XLA Modules:
  0.0 31.4 jit_solution(9959734707723630957)
XLA Ops:
  1.3 28.4 %shard_map.112 = (bf16[2,1,64,640]{3,2,1,0:T(8,128)(2,1)}, bf16[2,1,64,640]{3,2,1,0:T(8,128)(2,1)}, f32[2,2,1,2,16]{4,3,2,1,0:T(2,128)}) custom-call(s32[1,1]{1,0:T(1,128)} %bitcast.1.t_hbm, bf16[2,1,64,640]{3,2,1,0:T(8,128)(2,1)} %lat_hbm.1, bf16[2,1,64,640]{3,2,1,0:T(8,128)(2,1)} %stale_hbm.1, f32[2,2,1,2,16]{4,3,2,1,0:T(2,128)} %ssum_hbm.1, ...), custom_call_target="tpu_custom_call" | custom-call | tf_op jit(solution)/shard_map/pallas_call | solution.py:596
  29.7 1.7 %shard_map.113 = (bf16[2,1,64,640]{3,2,1,0:T(8,128)(2,1)}, bf16[2,1,64,640]{3,2,1,0:T(8,128)(2,1)}, f32[2,2,1,2,16]{4,3,2,1,0:T(2,128)}) custom-call(bf16[2,1,64,640]{3,2,1,0:T(8,128)(2,1)} %get-tuple-element.6.block_in, bf16[2,1,64,640]{3,2,1,0:T(8,128)(2,1)} %get-tuple-element.7.states_in, f32[2,2,1,2,16]{4,3,2,1,0:T(2,128)} %get-tuple-element.8.sums_in), custom_call_target="tpu_custom_call" | custom-call | tf_op jit(solution)/shard_map/pallas_call | solution.py:644
